TPU v7x, 32 devices: a whole 2x2x4 slice. The times are simulated.
32 devices in a mesh: client: 8 (over z, x), head: 4 (over y, core).
Axes of the slice: x: 2, y: 2, z: 4, core: 2. Of those that a mesh axis runs over, the one named last changes fastest.
Arguments:
- pre: bfloat16 [10240, 4096], P('client'), may hold values from -40 to 40
- delta: float32 [10240, 4096], P('client', 'head'), may hold values from -300 to 300
- head_weight: bfloat16 [4096, 4096], P(None, 'head'), may hold values from -0.09375 to 0.09375
- client_ids: int32 [128], P('client'), may hold values from 0 to 127, as said below
Outputs:
- head_grad: float32 [4096, 4096], P('client', 'head')
- bias_grad: float32 [4096], P('head')
- embed_grad: float32 [128, 4096], P('client', 'head')
- span_grad: float32 [80, 4096], P(None, 'head')
Inputs may be any that keep to these rules, and one draw needn't show every extreme that they name: `client_ids`: each of the 128 clients appears exactly once.
All inputs are finite; a program needn't handle non-finite values.
Results may differ from a plain program's by a relative error of at most 0.024.
Values may be sent and summed in bfloat16 or wider, within the bound.
A program may use at most 128 MiB of HBM per device.

v0:
```python
import jax
import jax.numpy as jnp
from jax import lax
from jax.sharding import PartitionSpec as P

EPSILON = 1e-06


def silu_slope(values):
    sigma = jax.nn.sigmoid(values)
    return sigma * (1.0 + values * (1.0 - sigma))


def clip_factor(total, number):
    return jnp.minimum(1.0, 1.0 / jnp.sqrt(total / number + EPSILON))


def per_device(pre, delta, head_weight, client_ids):
    rows_here, hidden_width = pre.shape
    emit_here = delta.shape[1]
    clients_here = client_ids.shape[0]
    span_count = rows_here // clients_here
    head_devices = lax.axis_size("head")
    client_devices = lax.axis_size("client")
    hidden = jax.nn.silu(pre.astype(jnp.float32)).astype(jnp.bfloat16)
    delta_low = delta.astype(jnp.bfloat16)
    head_raw = lax.psum_scatter(
        lax.dot_general(
            hidden, delta_low, (((0,), (0,)), ((), ())), preferred_element_type=jnp.float32
        ).astype(jnp.bfloat16),
        "client",
        scatter_dimension=0,
        tiled=True,
    ).astype(jnp.float32)
    head_square = jnp.sum(head_raw * head_raw)
    head_square = lax.psum(head_square, ("client", "head"))
    bias_local = jnp.sum(delta, axis=0)
    partial_sum = lax.dot_general(
        delta_low, head_weight, (((1,), (1,)), ((), ())), preferred_element_type=jnp.float32
    )
    rounded = lax.optimization_barrier(partial_sum.astype(jnp.bfloat16))
    block_grad = rounded.astype(jnp.float32) * silu_slope(pre.astype(jnp.float32))
    grouped = block_grad.reshape(clients_here, span_count, hidden_width)
    client_whole = jnp.sum(grouped, axis=1)
    span_whole = jnp.sum(grouped, axis=0)
    client_part, span_part = (
        lax.psum_scatter(
            client_whole.astype(jnp.bfloat16), "head", scatter_dimension=1, tiled=True
        ).astype(jnp.float32),
        lax.psum_scatter(
            span_whole.astype(jnp.bfloat16), "head", scatter_dimension=1, tiled=True
        ).astype(jnp.float32),
    )
    span_raw, bias_raw = (
        lax.psum(span_part.astype(jnp.bfloat16), "client").astype(jnp.float32),
        lax.psum(bias_local.astype(jnp.bfloat16), "client").astype(jnp.float32),
    )
    targets = lax.iota(jnp.int32, lax.axis_size("client") * clients_here)
    selector = (targets[:, None] == client_ids[None, :]).astype(jnp.float32)
    embed_raw = lax.psum_scatter(
        jnp.dot(
            selector,
            client_part,
            precision=lax.Precision.HIGHEST,
            preferred_element_type=jnp.float32,
        ).astype(jnp.bfloat16),
        "client",
        scatter_dimension=0,
        tiled=True,
    ).astype(jnp.float32)
    leading = (lax.axis_index("client") == 0).astype(jnp.float32)
    small_square = leading * (jnp.sum(span_raw * span_raw) + jnp.sum(bias_raw * bias_raw))
    embed_square = jnp.sum(embed_raw * embed_raw)
    embed_total, small_total = lax.psum((embed_square, small_square), ("client", "head"))
    emit_total = emit_here * head_devices
    clients_total = clients_here * client_devices
    head_factor = clip_factor(head_square, hidden_width * emit_total)
    embed_factor = clip_factor(embed_total, clients_total * hidden_width)
    rest_factor = clip_factor(small_total, span_count * hidden_width + emit_total)
    return (
        head_factor * head_raw,
        rest_factor * bias_raw,
        embed_factor * embed_raw,
        rest_factor * span_raw,
    )


def solution(mesh):
    placed = (P("client", None), P("client", "head"), P(None, "head"), P("client"))
    return jax.shard_map(
        per_device,
        mesh=mesh,
        in_specs=placed,
        out_specs=(P("client", "head"), P("head"), P("client", "head"), P(None, "head")),
        check_vma=False,
    )
```

profile of v0, /device:TPU:0, one launch (start us, length us, event | category | flops | bytes accessed | tf_op | source)
XLA Modules:
  0.0 433.6 jit_solution(12990887152646815512)
XLA Ops:
  7.2 0.0 reduce-scatter.9.cloned.1.call-start
  7.2 0.0 copy-start
  7.2 17.6 %convolution_convert_fusion = bf16[1280,4096]{1,0:T(8,128)(2,1)} fusion(bf16[4096,1024]{1,0:T(8,128)(2,1)} %param.6, f32[1280,1024]{1,0:T(8,128)} %param.5), kind=kOutput, calls=%fused_computation.10 | convolution fusion | flops 10743971840 | bytes 24117248 | tf_op jit(solution)/shard_map/dot_general | solution.py:38
  24.8 0.0 copy-done
  24.8 9.6 %fusion.6 = f32[1280,4096]{1,0:T(8,128)S(1)} fusion(bf16[1280,4096]{1,0:T(8,128)(2,1)S(1)} %copy-done, bf16[1280,4096]{1,0:T(8,128)(2,1)} %convolution_convert_fusion), kind=kLoop, calls=%fused_computation.9 | loop fusion | flops 52428800 | bytes 41943040 | tf_op jit(solution)/shard_map/mul | solution.py:42
  34.4 0.0 copy-start.1
  34.4 5.2 %fusion.20 = (bf16[16,4096]{1,0:T(8,128)(2,1)}, bf16[80,4096]{1,0:T(8,128)(2,1)}) fusion(f32[16,80,4096]{2,1,0:T(8,128)S(1)} %bitcast.3), kind=kLoop, calls=%fused_computation.31 | loop fusion | flops 10092544 | bytes 21757952 | tf_op jit(solution)/shard_map/reduce_sum | solution.py:44
  39.5 0.0 reduce-scatter.9.cloned.1.call-update
  39.6 0.0 reduce-scatter.7.cloned.1.call-start
  39.6 0.7 reduce-scatter.7.cloned.1.call-update
  40.3 0.0 reduce-scatter.11.cloned.1.call-start
  40.4 21.7 %reduce-scatter.9.cloned.1.call-done = bf16[16,1024]{1,0:T(8,128)(2,1)} async-done(((bf16[16,4096]{1,0:T(8,128)(2,1)}), bf16[16,1024]{1,0:T(8,128)(2,1)}) %reduce-scatter.9.cloned.1.call-update) | async-done | bytes 32784 | tf_op jit(solution)/shard_map/reduce_scatter | solution.py:47
  62.1 0.0 copy-done.1
  62.1 1.7 convolution_convert_fusion.1
  63.7 0.0 reduce-scatter.11.cloned.1.call-update
  63.8 0.0 all-reduce.3.cloned.1.call-start
  63.8 23.8 %reduce-scatter.7.cloned.1.call-done = bf16[80,1024]{1,0:T(8,128)(2,1)} async-done(((bf16[80,4096]{1,0:T(8,128)(2,1)}), bf16[80,1024]{1,0:T(8,128)(2,1)}) %reduce-scatter.7.cloned.1.call-update) | async-done | bytes 163856 | tf_op jit(solution)/shard_map/reduce_scatter | solution.py:50
  87.6 0.0 all-reduce.3.cloned.1.call-update
  87.6 0.2 reduce-scatter.5.cloned.1.call-start
  87.9 18.3 %fusion.9 = bf16[4096,1024]{1,0:T(8,128)(2,1)} fusion(bf16[1280,4096]{1,0:T(8,128)(2,1)} %param.4, f32[1280,1024]{1,0:T(8,128)} %param.5), kind=kOutput, calls=%fused_computation.12 | convolution fusion | flops 10774380544 | bytes 24117248 | tf_op jit(solution)/shard_map/dot_general | solution.py:28
  106.1 0.0 reduce-scatter.5.cloned.1.call-update
  106.2 2.9 reduce_sum.66
  109.0 21.5 %psum.37 = bf16[1024]{0:T(1024)(128)(2,1)S(1)} all-reduce(bf16[1024]{0:T(1024)(128)(2,1)S(1)} %reduce_sum.66), channel_id=1, replica_groups=mesh['client'=8,'head'=4] {'client'}, use_global_device_ids=true, to_apply=%region_8.9 | all-reduce | flops 1024 | bytes 4096 | tf_op jit(solution)/shard_map/psum | solution.py:56
  130.5 0.6 fusion.18
  131.1 22.5 %reduce-scatter.11.cloned.1.call-done = bf16[16,1024]{1,0:T(8,128)(2,1)} async-done(((bf16[128,1024]{1,0:T(8,128)(2,1)}), bf16[16,1024]{1,0:T(8,128)(2,1)}) %reduce-scatter.11.cloned.1.call-update) | async-done | bytes 32784 | tf_op jit(solution)/shard_map/reduce_scatter | solution.py:60
  153.6 1.4 fusion.16
  155.0 70.9 %all-reduce.3.cloned.1.call-done = bf16[80,1024]{1,0:T(8,128)(2,1)} async-done(((bf16[80,1024]{1,0:T(8,128)(2,1)}), bf16[80,1024]{1,0:T(8,128)(2,1)}) %all-reduce.3.cloned.1.call-update) | async-done | bytes 163856 | tf_op jit(solution)/shard_map/psum | solution.py:55
  225.9 1.6 fusion.15
  228.8 147.9 %reduce-scatter.5.cloned.1.call-done = bf16[512,1024]{1,0:T(8,128)(2,1)} async-done(((bf16[4096,1024]{1,0:T(8,128)(2,1)}), bf16[512,1024]{1,0:T(8,128)(2,1)}) %reduce-scatter.5.cloned.1.call-update) | async-done | bytes 1048592 | tf_op jit(solution)/shard_map/reduce_scatter | solution.py:27
  376.7 2.4 fusion.12
  379.0 39.5 %all-reduce = (f32[]{:T(128)}, f32[]{:T(128)}, f32[]{:T(128)}) all-reduce(f32[]{:T(128)} %fusion.12, f32[]{:T(128)S(6)} %mul.61, f32[]{:T(128)} %fusion.16), channel_id=1, replica_groups=mesh['client'=8,'head'=4] {'client','head'}, use_global_device_ids=true, to_apply=%region_2.3 | all-reduce | flops 3 | bytes 24 | tf_op jit(solution)/shard_map/psum | solution.py:36
  419.9 0.6 convert_multiply_fusion.8
  421.2 1.7 convert_multiply_fusion.4
  422.9 1.4 convert_multiply_fusion.6
  424.3 2.8 convert_multiply_fusion.2
Async XLA Ops:
  7.2 54.9 %reduce-scatter.9.cloned.1.call-start = ((), (), s32[]{:S(2)}) async-start(), calls=%async_computation.7 | async-start | bytes 163840 | tf_op jit(solution)/shard_map/reduce_scatter | solution.py:47
  7.2 17.6 %copy-start = (bf16[1280,4096]{1,0:T(8,128)(2,1)S(1)}, bf16[1280,4096]{1,0:T(8,128)(2,1)}, u32[]{:S(2)}) copy-start(bf16[1280,4096]{1,0:T(8,128)(2,1)} %param.4) | copy-start | bytes 31457284
  34.4 27.7 %copy-start.1 = (s32[16]{0:T(128)S(1)}, s32[16]{0:T(128)}, u32[]{:S(2)}) copy-start(s32[16]{0:T(128)} %param.7) | copy-start | bytes 196
  39.6 48.0 %reduce-scatter.7.cloned.1.call-start = ((), (), s32[]{:S(2)}) async-start(), calls=%async_computation.5 | async-start | bytes 819200 | tf_op jit(solution)/shard_map/reduce_scatter | solution.py:50
  40.3 113.3 %reduce-scatter.11.cloned.1.call-start = ((), (), s32[]{:S(2)}) async-start(), calls=%async_computation.8 | async-start | bytes 294912 | tf_op jit(solution)/shard_map/reduce_scatter | solution.py:60
  63.8 162.1 %all-reduce.3.cloned.1.call-start = ((), (), s32[]{:S(2)}) async-start(), calls=%async_computation.6 | async-start | bytes 327680 | tf_op jit(solution)/shard_map/psum | solution.py:55
  87.6 289.0 %reduce-scatter.5.cloned.1.call-start = ((), (), s32[]{:S(2)}) async-start(), calls=%async_computation.4 | async-start | bytes 9437184 | tf_op jit(solution)/shard_map/reduce_scatter | solution.py:27
Sparse Core Ops, SparseCore 0:
  39.7 22.3 reduce-scatter.8
  65.1 22.4 reduce-scatter.6
  91.5 62.0 reduce-scatter.10
  156.8 69.0 all-reduce.2
  229.3 147.2 reduce-scatter.4
where the time goes:
time: 434 us
  waiting for transfers between devices  288 us (66%)
  blocking collectives  61 us (14%)
  matrix products  37.5 us (9%)
  other arithmetic  30 us (7%)
  between operations  17.2 us (4%)
    reduce_scatter x1, waiting for transfers between devices, per_device(): lax.psum_scatter(lax.dot_general(hidden, delta_low, (((0,), (0,)), ((), (...  148 us
    psum x1, waiting for transfers between devices, per_device(): lax.psum(span_part.astype(jnp.bfloat16), 'client').astype(jnp.float32)  70.9 us
    psum x1, blocking collectives, per_device(): head_square = lax.psum(head_square, ('client', 'head'))  39.5 us
    reduce_scatter x1, waiting for transfers between devices, per_device(): lax.psum_scatter(span_whole.astype(jnp.bfloat16), 'head', scatter_dimensi...  23.8 us
    reduce_scatter x1, waiting for transfers between devices, per_device(): lax.psum_scatter(jnp.dot(selector, client_part, precision=lax.Precision.H...  22.5 us
    reduce_scatter x1, waiting for transfers between devices, per_device(): lax.psum_scatter(client_whole.astype(jnp.bfloat16), 'head', scatter_dimen...  21.7 us
    psum x1, blocking collectives, per_device(): lax.psum(bias_local.astype(jnp.bfloat16), 'client').astype(jnp.float32)  21.5 us
    dot_general x1, matrix products, per_device(): lax.dot_general(hidden, delta_low, (((0,), (0,)), ((), ())), preferred_el...  18.3 us
  transfers between devices with their start and end apart: 5, of which 5 were waited for; matrix products, arithmetic and copies ran while one was open for 6% of the time, Pallas kernels for 0%

commit v1 on v0

--- a/solution.py
+++ b/solution.py
@@ -1,9 +1,19 @@
+import functools
 import jax
 import jax.numpy as jnp
 from jax import lax
 from jax.sharding import PartitionSpec as P
 
 EPSILON = 1e-06
+
+
+def solve_masks_on_mesh(load, a_name, peer_axis):
+    for ii in (a_name, peer_axis):
+        load = lax.psum(load, ii)
+    return load
+
+
+make_boxes = functools.partial(solve_masks_on_mesh, a_name="head", peer_axis="client")
 
 
 def silu_slope(values):
@@ -33,7 +43,7 @@
         tiled=True,
     ).astype(jnp.float32)
     head_square = jnp.sum(head_raw * head_raw)
-    head_square = lax.psum(head_square, ("client", "head"))
+    head_square = make_boxes(head_square)
     bias_local = jnp.sum(delta, axis=0)
     partial_sum = lax.dot_general(
         delta_low, head_weight, (((1,), (1,)), ((), ())), preferred_element_type=jnp.float32

time: 434 us -> 420 us (0.968)
  waiting for transfers between devices: 288 us -> 241 us
  blocking collectives: 61 us -> 93.3 us
    reduce_scatter x1, waiting for transfers between devices: 148 us -> 102 us  [per_device(): lax.psum_scatter(lax.dot_general(hidden, delta_low, (((0,), (0,)), ((), (...]
    psum x1 -> x3, blocking collectives: 39.5 us -> 71.8 us  [the longest x1 44.3 us: per_device(): lax.psum((embed_square, small_square), ('client', 'head'))]
  transfers between devices with their start and end apart: 5 -> 5, of which waited for: 5 -> 5; matrix products, arithmetic and copies ran while one was open for 6% -> 7% of each run, Pallas kernels for 0% -> 0%
where the time goes in v1:
time: 420 us
  waiting for transfers between devices  241 us (57%)
  blocking collectives  93.3 us (22%)
  matrix products  37.5 us (9%)
  other arithmetic  30 us (7%)
  between operations  17.2 us (4%)
    reduce_scatter x1, waiting for transfers between devices, per_device(): lax.psum_scatter(lax.dot_general(hidden, delta_low, (((0,), (0,)), ((), (...  102 us
    psum x1, waiting for transfers between devices, per_device(): lax.psum(span_part.astype(jnp.bfloat16), 'client').astype(jnp.float32)  70.9 us
    psum x1, blocking collectives, per_device(): lax.psum((embed_square, small_square), ('client', 'head'))  44.3 us
    psum x2, blocking collectives, solve_masks_on_mesh(): load = lax.psum(load, ii)  27.5 us
    reduce_scatter x1, waiting for transfers between devices, per_device(): lax.psum_scatter(span_whole.astype(jnp.bfloat16), 'head', scatter_dimensi...  23.8 us
    reduce_scatter x1, waiting for transfers between devices, per_device(): lax.psum_scatter(jnp.dot(selector, client_part, precision=lax.Precision.H...  22.5 us
    reduce_scatter x1, waiting for transfers between devices, per_device(): lax.psum_scatter(client_whole.astype(jnp.bfloat16), 'head', scatter_dimen...  21.7 us
    psum x1, blocking collectives, per_device(): lax.psum(bias_local.astype(jnp.bfloat16), 'client').astype(jnp.float32)  21.5 us
  transfers between devices with their start and end apart: 5, of which 5 were waited for; matrix products, arithmetic and copies ran while one was open for 7% of the time, Pallas kernels for 0%

profile of v1, /device:TPU:0, one launch (start us, length us, event | category | flops | bytes accessed | tf_op | source)
XLA Modules:
  0.0 419.7 jit_solution(8034545761507809878)
XLA Ops:
  7.2 0.0 reduce-scatter.9.cloned.1.call-start
  7.2 0.0 copy-start
  7.2 17.6 %convolution_convert_fusion = bf16[1280,4096]{1,0:T(8,128)(2,1)} fusion(bf16[4096,1024]{1,0:T(8,128)(2,1)} %param.6, f32[1280,1024]{1,0:T(8,128)} %param.5), kind=kOutput, calls=%fused_computation.10 | convolution fusion | flops 10743971840 | bytes 24117248 | tf_op jit(solution)/shard_map/dot_general | solution.py:48
  24.8 0.0 copy-done
  24.8 9.6 %fusion.6 = f32[1280,4096]{1,0:T(8,128)S(1)} fusion(bf16[1280,4096]{1,0:T(8,128)(2,1)S(1)} %copy-done, bf16[1280,4096]{1,0:T(8,128)(2,1)} %convolution_convert_fusion), kind=kLoop, calls=%fused_computation.9 | loop fusion | flops 52428800 | bytes 41943040 | tf_op jit(solution)/shard_map/mul | solution.py:52
  34.4 0.0 copy-start.1
  34.4 5.2 %fusion.20 = (bf16[16,4096]{1,0:T(8,128)(2,1)}, bf16[80,4096]{1,0:T(8,128)(2,1)}) fusion(f32[16,80,4096]{2,1,0:T(8,128)S(1)} %bitcast.3), kind=kLoop, calls=%fused_computation.31 | loop fusion | flops 10092544 | bytes 21757952 | tf_op jit(solution)/shard_map/reduce_sum | solution.py:54
  39.5 0.0 reduce-scatter.9.cloned.1.call-update
  39.6 0.0 reduce-scatter.7.cloned.1.call-start
  39.6 0.7 reduce-scatter.7.cloned.1.call-update
  40.3 0.0 reduce-scatter.11.cloned.1.call-start
  40.4 21.7 %reduce-scatter.9.cloned.1.call-done = bf16[16,1024]{1,0:T(8,128)(2,1)} async-done(((bf16[16,4096]{1,0:T(8,128)(2,1)}), bf16[16,1024]{1,0:T(8,128)(2,1)}) %reduce-scatter.9.cloned.1.call-update) | async-done | bytes 32784 | tf_op jit(solution)/shard_map/reduce_scatter | solution.py:57
  62.1 0.0 copy-done.1
  62.1 1.7 convolution_convert_fusion.1
  63.7 0.0 reduce-scatter.11.cloned.1.call-update
  63.8 0.0 all-reduce.3.cloned.1.call-start
  63.8 23.8 %reduce-scatter.7.cloned.1.call-done = bf16[80,1024]{1,0:T(8,128)(2,1)} async-done(((bf16[80,4096]{1,0:T(8,128)(2,1)}), bf16[80,1024]{1,0:T(8,128)(2,1)}) %reduce-scatter.7.cloned.1.call-update) | async-done | bytes 163856 | tf_op jit(solution)/shard_map/reduce_scatter | solution.py:60
  87.6 0.0 all-reduce.3.cloned.1.call-update
  87.6 0.2 reduce-scatter.5.cloned.1.call-start
  87.9 18.3 %fusion.9 = bf16[4096,1024]{1,0:T(8,128)(2,1)} fusion(bf16[1280,4096]{1,0:T(8,128)(2,1)} %param.4, f32[1280,1024]{1,0:T(8,128)} %param.5), kind=kOutput, calls=%fused_computation.12 | convolution fusion | flops 10774380544 | bytes 24117248 | tf_op jit(solution)/shard_map/dot_general | solution.py:38
  106.1 0.0 reduce-scatter.5.cloned.1.call-update
  106.2 2.9 reduce_sum.66
  109.0 21.5 %psum.45 = bf16[1024]{0:T(1024)(128)(2,1)S(1)} all-reduce(bf16[1024]{0:T(1024)(128)(2,1)S(1)} %reduce_sum.66), channel_id=1, replica_groups=mesh['client'=8,'head'=4] {'client'}, use_global_device_ids=true, to_apply=%region_9.10 | all-reduce | flops 1024 | bytes 4096 | tf_op jit(solution)/shard_map/psum | solution.py:66
  130.5 0.6 fusion.18
  131.1 22.5 %reduce-scatter.11.cloned.1.call-done = bf16[16,1024]{1,0:T(8,128)(2,1)} async-done(((bf16[128,1024]{1,0:T(8,128)(2,1)}), bf16[16,1024]{1,0:T(8,128)(2,1)}) %reduce-scatter.11.cloned.1.call-update) | async-done | bytes 32784 | tf_op jit(solution)/shard_map/reduce_scatter | solution.py:70
  153.6 1.4 fusion.16
  155.0 70.9 %all-reduce.3.cloned.1.call-done = bf16[80,1024]{1,0:T(8,128)(2,1)} async-done(((bf16[80,1024]{1,0:T(8,128)(2,1)}), bf16[80,1024]{1,0:T(8,128)(2,1)}) %all-reduce.3.cloned.1.call-update) | async-done | bytes 163856 | tf_op jit(solution)/shard_map/psum | solution.py:65
  225.9 1.6 fusion.15
  228.8 44.3 %all-reduce = (f32[]{:T(128)}, f32[]{:T(128)}) all-reduce(f32[]{:T(128)S(6)} %mul.61, f32[]{:T(128)} %fusion.16), channel_id=1, replica_groups=mesh['client'=8,'head'=4] {'client','head'}, use_global_device_ids=true, to_apply=%region_11.12 | all-reduce | flops 2 | bytes 16 | tf_op jit(solution)/shard_map/psum | solution.py:84
  274.5 1.7 convert_multiply_fusion.4
  276.1 101.6 %reduce-scatter.5.cloned.1.call-done = bf16[512,1024]{1,0:T(8,128)(2,1)} async-done(((bf16[4096,1024]{1,0:T(8,128)(2,1)}), bf16[512,1024]{1,0:T(8,128)(2,1)}) %reduce-scatter.5.cloned.1.call-update) | async-done | bytes 1048592 | tf_op jit(solution)/shard_map/reduce_scatter | solution.py:37
  377.7 2.4 fusion.12
  380.1 1.4 convert_multiply_fusion.6
  381.5 6.9 %psum.42 = f32[]{:T(128)} all-reduce(f32[]{:T(128)} %fusion.12), channel_id=1, replica_groups=mesh['client'=8,'head'=4] {'head'}, use_global_device_ids=true, to_apply=%region_2.3 | all-reduce | flops 1 | bytes 8 | tf_op jit(solution)/shard_map/psum | solution.py:12
  388.3 0.6 convert_multiply_fusion.8
  388.9 20.7 %psum.43 = f32[]{:T(128)} all-reduce(f32[]{:T(128)} %psum.42), channel_id=1, replica_groups=mesh['client'=8,'head'=4] {'client'}, use_global_device_ids=true, to_apply=%region_3.4 | all-reduce | flops 1 | bytes 8 | tf_op jit(solution)/shard_map/psum | solution.py:12
  410.3 2.8 convert_multiply_fusion.2
Async XLA Ops:
  7.2 54.9 %reduce-scatter.9.cloned.1.call-start = ((), (), s32[]{:S(2)}) async-start(), calls=%async_computation.7 | async-start | bytes 163840 | tf_op jit(solution)/shard_map/reduce_scatter | solution.py:57
  7.2 17.6 %copy-start = (bf16[1280,4096]{1,0:T(8,128)(2,1)S(1)}, bf16[1280,4096]{1,0:T(8,128)(2,1)}, u32[]{:S(2)}) copy-start(bf16[1280,4096]{1,0:T(8,128)(2,1)} %param.4) | copy-start | bytes 31457284
  34.4 27.7 %copy-start.1 = (s32[16]{0:T(128)S(1)}, s32[16]{0:T(128)}, u32[]{:S(2)}) copy-start(s32[16]{0:T(128)} %param.7) | copy-start | bytes 196
  39.6 48.0 %reduce-scatter.7.cloned.1.call-start = ((), (), s32[]{:S(2)}) async-start(), calls=%async_computation.5 | async-start | bytes 819200 | tf_op jit(solution)/shard_map/reduce_scatter | solution.py:60
  40.3 113.3 %reduce-scatter.11.cloned.1.call-start = ((), (), s32[]{:S(2)}) async-start(), calls=%async_computation.8 | async-start | bytes 294912 | tf_op jit(solution)/shard_map/reduce_scatter | solution.py:70
  63.8 162.1 %all-reduce.3.cloned.1.call-start = ((), (), s32[]{:S(2)}) async-start(), calls=%async_computation.6 | async-start | bytes 327680 | tf_op jit(solution)/shard_map/psum | solution.py:65
  87.6 290.1 %reduce-scatter.5.cloned.1.call-start = ((), (), s32[]{:S(2)}) async-start(), calls=%async_computation.4 | async-start | bytes 9437184 | tf_op jit(solution)/shard_map/reduce_scatter | solution.py:37
Sparse Core Ops, SparseCore 0:
  39.7 22.3 reduce-scatter.8
  65.1 22.4 reduce-scatter.6
  91.5 62.0 reduce-scatter.10
  156.8 69.0 all-reduce.2
  229.3 148.3 reduce-scatter.4
